TPU v7x, 32 devices: a whole 2x2x4 slice. The times are simulated.
32 devices in a mesh: groups: 2 (over y), ctx: 4 (over z), role: 2 (over x), seq: 2 (over core).
Axes of the slice: x: 2, y: 2, z: 4, core: 2. Of those that a mesh axis runs over, the one named last changes fastest.
Arguments:
- queries: bfloat16 [32, 128, 576], P(('groups', 'role', 'seq'), 'ctx'), parts along dimension 0, may hold values from -24 to 24
- cache: bfloat16 [16, 4096, 576], P(('groups', 'role', 'seq'), 'ctx'), parts along dimension 0, may hold values from -4 to 4
- lengths: int32 [16], P(('groups', 'role', 'seq')), parts along dimension 0, may hold values from 4 to 4096, as said below
- positions: int32 [32], P(('groups', 'role', 'seq')), parts along dimension 0, may hold values from 0 to 4098, as said below
- value_up_weight: bfloat16 [128, 512, 128], P('ctx', ('role', 'seq')), may hold values from -0.25 to 0.25
- out_proj: bfloat16 [16384, 7168], P('ctx', ('role', 'seq')), may hold values from -0.046875 to 0.046875
- residual: bfloat16 [32, 7168], P('groups', ('role', 'seq')), parts along dimension 0, may hold values from -4 to 4
- norm_gain: float32 [7168], P(('role', 'seq')), may hold values from 0.5 to 1.5
- gate_weight: bfloat16 [7168, 9216], P(('role', 'seq'), 'ctx'), may hold values from -0.0625 to 0.0625
- up_weight: bfloat16 [7168, 9216], P(('role', 'seq'), 'ctx'), may hold values from -0.0625 to 0.0625
- down_weight: bfloat16 [9216, 7168], P('ctx', ('role', 'seq')), may hold values from -0.0625 to 0.0625
Outputs:
- layer_out: bfloat16 [32, 7168], P(('groups', 'ctx'), ('role', 'seq')), parts along dimension 0
There are 2 independent parts, one for each index of `groups`. A program takes and returns all parts, laid end to end along the dimension named above; an argument that names none is the same for every part. Nothing has to cross between parts.
Inputs may be any that keep to these rules, and one draw needn't show every extreme that they name: `lengths`: every sequence has at least 4 cached positions, and in every draw some sequence has all 4096. positions[r] lies between lengths[r // 2] - 4 and lengths[r // 2] + 2.
All inputs are finite; a program needn't handle non-finite values.
Results may differ from a plain program's by a relative error of at most 0.013.
Values may be sent and summed in bfloat16 or wider, within the bound.
A program may use at most 128 MiB of HBM per device.

v0:
```python
import functools

import jax
import jax.numpy as jnp
from jax import lax
from jax.experimental import pallas as pl
from jax.experimental.pallas import tpu as pltpu
from jax.sharding import PartitionSpec as P

D = 7168
LATENT = 512
MTP = 2

softmax_scale = 0.07216878364870323
epsilon = 1e-06
MESH = pl.DeviceIdType.MESH
VMEM_BYTES = 60 * 1024 * 1024
f32, bf16 = jnp.float32, jnp.bfloat16


def ctx_group(n):
    me = lax.axis_index("ctx")

    def peer(d):
        k = lax.rem(me + d, n)
        return k, {"ctx": k}

    return me, peer


def feature_group(n_role, n_seq):
    n = n_role * n_seq
    me = lax.axis_index("role") * n_seq + lax.axis_index("seq")

    def peer(d):
        k = lax.rem(me + d, n)
        return k, {"role": k // n_seq, "seq": lax.rem(k, n_seq)}

    return me, peer


def enter(groups):
    barrier = pltpu.get_barrier_semaphore()
    count = 0
    for n, peer in groups:
        for d in range(1, n):
            pl.semaphore_signal(barrier, inc=1, device_id=peer(d)[1], device_id_type=MESH)
            count += 1
    pl.semaphore_wait(barrier, count)


def remote(src, dst, send, recv, device):
    return pltpu.make_async_remote_copy(
        src_ref=src, dst_ref=dst, send_sem=send, recv_sem=recv,
        device_id=device, device_id_type=MESH,
    )


def attend(n, n_role, n_seq, q_ref, cache_ref, cache_copy, len_ref, pos_ref, out_ref,
           q_all, o_send, o_recv, s_send, s_recv, a_send, sems):
    nr = n_role * n_seq
    me, peer = ctx_group(n)
    fme, fpeer = feature_group(n_role, n_seq)
    seqs, _, context = cache_ref.shape
    rows = q_ref.shape[1]
    heads = rows // MTP

    q_copies = []
    for s in range(seqs):
        for d in range(1, n):
            c = remote(q_ref.at[s], q_all.at[me, s], sems.at[s, d], sems.at[seqs + s, d],
                       peer(d)[1])
            c.start()
            q_copies.append(c)

    places = me * context + lax.broadcasted_iota(jnp.int32, (rows, context), 1)
    first = lax.broadcasted_iota(jnp.int32, (rows, context), 0) < heads
    lives = []
    for s in range(seqs):
        limit = jnp.where(first, pos_ref[MTP * s], pos_ref[MTP * s + 1])
        lives.append((places < len_ref[s]) & (places <= limit))

    lane = lax.broadcasted_iota(jnp.int32, (rows, 128), 1)

    def block(q, s):
        keys = cache_ref[s]
        scores = jnp.dot(q, keys, preferred_element_type=f32) * softmax_scale
        live = lives[s]
        top = jnp.max(jnp.where(live, scores, -1e30), axis=1, keepdims=True)
        probs = jnp.exp(jnp.where(live, scores - top, -1e30)).astype(bf16)
        total = jnp.sum(probs.astype(f32), axis=1, keepdims=True)
        out = lax.dot_general(
            probs, keys[:LATENT], (((1,), (1,)), ((), ())), preferred_element_type=f32)
        return out, top, total

    cache_copy.wait()
    own = [block(q_ref[s], s) for s in range(seqs)]
    o_copies, s_copies = {}, {}
    for s in range(seqs):
        for d in range(1, n):
            src, device = peer(n - d)
            remote(q_ref.at[s], q_all.at[src, s], sems.at[s, d], sems.at[seqs + s, d],
                   device).wait_recv()
            o, top, total = block(q_all[src, s], s)
            o_send[d, s] = o.astype(bf16)
            s_send[d, s] = jnp.where(lane == 0, top, total).T[0:8]
            c = remote(o_send.at[d, s], o_recv.at[d, s], sems.at[2 * seqs + s, d],
                       sems.at[3 * seqs + s, d], device)
            c.start()
            o_copies[s, d] = c
            c = remote(s_send.at[d, s], s_recv.at[d, s], sems.at[4 * seqs + s, d],
                       sems.at[5 * seqs + s, d], device)
            c.start()
            s_copies[s, d] = c
    for c in q_copies:
        c.wait_send()

    heads = rows // MTP
    merged = []
    for s in range(seqs):
        own_o, top, total = own[s]
        tops, totals = [top], [total]
        for d in range(1, n):
            s_copies[s, d].wait()
            back = jnp.concatenate([s_recv[d, s]] * 16, axis=0).T
            tops.append(back[:, 0:1])
            totals.append(back[:, 1:2])
        highest = functools.reduce(jnp.maximum, tops)
        factors = [jnp.exp(t - highest) for t in tops]
        denom = sum(f * t for f, t in zip(factors, totals))
        numer = factors[0] * own_o
        for d in range(1, n):
            o_copies[s, d].wait()
            numer = numer + factors[d] * o_recv[d, s].astype(f32)
        merged.append((numer / denom).astype(bf16))

    part = LATENT // nr
    for k in range(nr):
        for r in range(seqs * MTP):
            t = r % MTP
            a_send[k, r] = merged[r // MTP][t * heads:(t + 1) * heads, k * part:(k + 1) * part]
    copies = []
    for d in range(1, nr):
        k, device = fpeer(d)
        c = remote(a_send.at[k], out_ref.at[fme], sems.at[6 * seqs, d], sems.at[7 * seqs, d], device)
        c.start()
        copies.append(c)
    out_ref[fme] = a_send[fme]
    for d in range(1, nr):
        k, device = fpeer(nr - d)
        copies[d - 1].wait_send()
        remote(a_send.at[k], out_ref.at[k], sems.at[6 * seqs, d], sems.at[7 * seqs, d],
               device).wait_recv()


def layer_kernel(n, n_role, n_seq, q_ref, cache_hbm, len_ref, pos_ref, vu_hbm, res_ref, gain_ref,
                 wo_hbm, wg_hbm, wu_hbm, wd_hbm,
                 out_ref, cache, vu, q_all, o_send, o_recv, s_send, s_recv, a_send, a_all, a_head,
                 mixed, pv_ref, wo, wg, wu, wd, pv_recv, v_send, v_all, v_full, acc, po_send,
                 po_recv, resid, xg_ref, g_acc, u_acc, gu_send, gu_recv, ss_send, ss_recv, h_send,
                 h_all, h_full, dn, dn_send, dn_recv, wsem, lsem, asems, sems):
    nr = n_role * n_seq
    me, peer = ctx_group(n)
    fme, fpeer = feature_group(n_role, n_seq)

    cache_copy = pltpu.make_async_copy(cache_hbm, cache, lsem.at[0])
    cache_copy.start()
    vu_copy = pltpu.make_async_copy(vu_hbm, vu, lsem.at[1])
    vu_copy.start()
    weights = []
    for which, (hbm, vmem) in enumerate(((wo_hbm, wo), (wg_hbm, wg), (wu_hbm, wu), (wd_hbm, wd))):
        depth = vmem.shape[1]

        def fetch(i, hbm=hbm, vmem=vmem, depth=depth, which=which):
            return pltpu.make_async_copy(
                hbm.at[pl.ds(i * depth, depth)], vmem.at[i], wsem.at[which, i])

        weights.append((fetch, vmem))
    for fetch, vmem in weights:
        for i in range(vmem.shape[0]):
            fetch(i).start()
    enter(((n, peer), (nr, fpeer)))
    attend(n, n_role, n_seq, q_ref, cache, cache_copy, len_ref, pos_ref, a_all,
           q_all, o_send, o_recv, s_send, s_recv, a_send, asems)
    rows, heads = a_all.shape[1:3]
    for j in range(nr):
        for r in range(rows):
            a_head[:, j * rows + r, :] = a_all[j, r].astype(f32)
    vu_copy.wait()
    vdim = vu.shape[2]
    for h in range(heads):
        mixed[:, h * vdim:(h + 1) * vdim] = jnp.dot(
            a_head[h].astype(bf16), vu[h], preferred_element_type=f32)
    for k in range(nr):
        pv_ref[k] = mixed[k * rows:(k + 1) * rows, :].astype(bf16)

    def matmul(x_ref, *pairs):
        chunks, depth, _ = weights[pairs[0][0]][1].shape
        for which, acc_ref in pairs:
            fetch, vmem = weights[which]
            fetch(0).wait()
            acc_ref[...] = jnp.dot(x_ref[:, :depth], vmem[0], preferred_element_type=f32)
        if chunks == 1:
            return

        @pl.loop(1, chunks)
        def _(i):
            x = x_ref[:, pl.ds(pl.multiple_of(i * depth, depth), depth)]
            for which, acc_ref in pairs:
                fetch, vmem = weights[which]
                fetch(i).wait()
                acc_ref[...] += jnp.dot(x, vmem[i], preferred_element_type=f32)

    def swap(size, peer_of, chunk, recv, row):
        copies = []
        for d in range(1, size):
            k, device = peer_of(d)
            c = remote(chunk(k), recv.at[d], sems.at[row, d], sems.at[row + 1, d], device)
            c.start()
            copies.append(c)
        return copies

    def gather(size, my, peer_of, send, full, row):
        copies = []
        for d in range(1, size):
            c = remote(send, full.at[my], sems.at[row, d], sems.at[row + 1, d], peer_of(d)[1])
            c.start()
            copies.append(c)
        full[my] = send[...]
        for d in range(1, size):
            k, device = peer_of(size - d)
            copies[d - 1].wait_send()
            remote(send, full.at[k], sems.at[row, d], sems.at[row + 1, d], device).wait_recv()

    part = res_ref.shape[0] // nr
    copies = swap(nr, fpeer, lambda k: pv_ref.at[k], pv_recv, 0)
    vals = pv_ref[fme].astype(f32)
    for d in range(1, nr):
        copies[d - 1].wait()
        vals = vals + pv_recv[d].astype(f32)
    v_send[...] = vals.astype(bf16)
    gather(nr, fme, fpeer, v_send, v_all, 2)
    for k in range(nr):
        acc_rows = v_all[k].astype(f32)
        v_full[k * part:(k + 1) * part, :] = acc_rows
    x_ref = xg_ref[0]
    x_ref[...] = v_full[...].astype(bf16)
    matmul(x_ref, (0, acc))

    po_send[...] = acc[...].astype(bf16)
    copies = swap(n, peer, lambda k: po_send, po_recv, 4)
    total = res_ref[...].astype(f32) + acc[...]
    for d in range(1, n):
        copies[d - 1].wait()
        total = total + po_recv[d].astype(f32)
    crows = res_ref.shape[0] // n
    for k in range(n):
        resid[k] = total[k * crows:(k + 1) * crows]
    sumsq = jnp.sum(total * total, axis=1, keepdims=True)
    sumsq = jnp.broadcast_to(sumsq, (total.shape[0], 128))
    for k in range(nr):
        ss_send[k] = sumsq[k * part:(k + 1) * part]
    s_copies = swap(nr, fpeer, lambda k: ss_send.at[k], ss_recv, 6)
    x_ref = xg_ref[1]
    x_ref[...] = (total * gain_ref[...]).astype(bf16)
    matmul(x_ref, (1, g_acc), (2, u_acc))

    for j, a in enumerate((g_acc, u_acc)):
        for k in range(nr):
            gu_send[k, j] = a[k * part:(k + 1) * part, :].astype(bf16)
    copies = swap(nr, fpeer, lambda k: gu_send.at[k], gu_recv, 8)
    ss = ss_send[fme]
    for d in range(1, nr):
        s_copies[d - 1].wait()
        ss = ss + ss_recv[d]
    inv = lax.rsqrt(ss[:, 0:1] / D + epsilon)
    gate = gu_send[fme, 0].astype(f32)
    up = gu_send[fme, 1].astype(f32)
    for d in range(1, nr):
        copies[d - 1].wait()
        gate = gate + gu_recv[d, 0].astype(f32)
        up = up + gu_recv[d, 1].astype(f32)
    gate = gate * inv
    up = up * inv
    h_send[...] = (gate / (1.0 + jnp.exp(-gate)) * up).astype(bf16)
    gather(nr, fme, fpeer, h_send, h_all, 10)
    for k in range(nr):
        h_full[k * part:(k + 1) * part, :] = h_all[k].astype(f32)
    x_ref = xg_ref[2]
    x_ref[...] = h_full[...].astype(bf16)
    matmul(x_ref, (3, acc))

    for k in range(n):
        piece = acc[k * crows:(k + 1) * crows, :]
        dn[k] = piece
        dn_send[k] = piece.astype(bf16)
    copies = swap(n, peer, lambda k: dn_send.at[k], dn_recv, 12)
    result = resid[me] + dn[me]
    for d in range(1, n):
        copies[d - 1].wait()
        result = result + dn_recv[d].astype(f32)
    out_ref[...] = result.astype(bf16)


def chunk_of(depth):
    for size in (1024, 768, 512, 256):
        if depth % size == 0:
            return size
    return depth


def per_device(sizes, queries, cache, lengths, positions, value_up_weight, out_proj, residual,
               norm_gain, gate_weight, up_weight, down_weight):
    n, n_role, n_seq = sizes
    nr = n_role * n_seq
    rows, heads, width = queries.shape
    seqs = cache.shape[0]
    span = rows * heads // seqs
    lat = LATENT // nr
    vmem = pl.BlockSpec(memory_space=pltpu.VMEM)
    smem = pl.BlockSpec(memory_space=pltpu.SMEM)
    hbm = pl.BlockSpec(memory_space=pl.ANY)
    most = max(n, nr)
    sems = lambda k: pltpu.SemaphoreType.DMA((k, most))
    vwide = heads * value_up_weight.shape[2]
    all_rows, dd = residual.shape
    ff = gate_weight.shape[1]
    part, crows = all_rows // nr, all_rows // n

    def held(w):
        size = chunk_of(w.shape[0])
        return pltpu.VMEM((w.shape[0] // size, size, w.shape[1]), bf16)

    ws = (out_proj, gate_weight, up_weight, down_weight)
    most_chunks = max(w.shape[0] // chunk_of(w.shape[0]) for w in ws)
    V = pltpu.VMEM
    return pl.pallas_call(
        functools.partial(layer_kernel, n, n_role, n_seq),
        out_shape=jax.ShapeDtypeStruct((crows, dd), bf16),
        in_specs=[vmem, hbm, smem, smem, hbm, vmem, vmem] + [hbm] * 4,
        out_specs=vmem,
        scratch_shapes=[
            V((cache.shape[0], width, cache.shape[1]), bf16),
            V(value_up_weight.shape, bf16),
            V((n, seqs, span, width), bf16),
            V((n, seqs, span, LATENT), bf16),
            V((n, seqs, span, LATENT), bf16),
            V((n, seqs, 8, span), f32),
            V((n, seqs, 8, span), f32),
            V((nr, rows, heads, lat), bf16),
            V((nr, rows, heads, lat), bf16),
            V((heads, all_rows, lat), f32),
            V((all_rows, vwide), f32),
            V((nr, part, vwide), bf16),
            *[held(w) for w in ws],
            V((nr, part, vwide), bf16),
            V((part, vwide), bf16),
            V((nr, part, vwide), bf16),
            V((all_rows, vwide), f32),
            V((all_rows, dd), f32),
            V((all_rows, dd), bf16),
            V((n, all_rows, dd), bf16),
            V((n, crows, dd), f32),
            [V((all_rows, vwide), bf16), V((all_rows, dd), bf16), V((all_rows, ff), bf16)],
            V((all_rows, ff), f32),
            V((all_rows, ff), f32),
            V((nr, 2, part, ff), bf16),
            V((nr, 2, part, ff), bf16),
            V((nr, part, 128), f32),
            V((nr, part, 128), f32),
            V((part, ff), bf16),
            V((nr, part, ff), bf16),
            V((all_rows, ff), f32),
            V((n, crows, dd), f32),
            V((n, crows, dd), bf16),
            V((n, crows, dd), bf16),
            pltpu.SemaphoreType.DMA((4, most_chunks)),
            pltpu.SemaphoreType.DMA((2,)),
            sems(8 * seqs),
            sems(14),
        ],
        compiler_params=pltpu.CompilerParams(
            collective_id=0, has_side_effects=True, vmem_limit_bytes=VMEM_BYTES),
        name="layer",
    )(queries.reshape(seqs, span, width), cache.transpose(0, 2, 1), lengths, positions, value_up_weight,
      residual, norm_gain.reshape(1, dd), *ws)


def solution(mesh):
    placed = (
        P(("groups", "role", "seq"), "ctx", None),
        P(("groups", "role", "seq"), "ctx", None),
        P(("groups", "role", "seq")),
        P(("groups", "role", "seq")),
        P("ctx", ("role", "seq"), None),
        P("ctx", ("role", "seq")),
        P("groups", ("role", "seq")),
        P(("role", "seq")),
        P(("role", "seq"), "ctx"),
        P(("role", "seq"), "ctx"),
        P("ctx", ("role", "seq")),
    )
    sizes = (mesh.shape["ctx"], mesh.shape["role"], mesh.shape["seq"])
    return jax.shard_map(
        functools.partial(per_device, sizes),
        mesh=mesh,
        in_specs=placed,
        out_specs=P(("groups", "ctx"), ("role", "seq")),
        check_vma=False,
    )
```

profile of v0, /device:TPU:0, one launch (start us, length us, event | category | flops | bytes accessed | tf_op | source)
XLA Modules:
  0.0 73.9 jit_solution(13575558870737305548)
XLA Ops:
  0.0 1.3 %reshape.7.gain_ref = f32[1,1792]{1,0:T(1,128)} reshape(f32[1792]{0:T(1024)} %param.18) | data formatting | bytes 14336 | tf_op jit(solution)/shard_map/reshape | solution.py:386
  1.3 71.2 %layer.1 = bf16[4,1792]{1,0:T(4,128)(2,1)} custom-call(bf16[2,64,576]{2,1,0:T(8,128)(2,1)} %bitcast.3, bf16[2,576,1024]{2,1,0:T(8,128)(2,1)} %bitcast.2, s32[2]{0:T(128)} %len_ref.1, s32[4]{0:T(128)} %pos_ref.1, bf16[32,128,128]{2,1,0:T(8,128)(2,1)} %vu_hbm.1, bf16[16,1792]{1,0:T(8,128)(2,1)} %res_ref.1, f32[1,1792]{1,0:T(1,128)} %reshape.7.gain_ref, ...), custom_call_target="tpu_custom_call" | custom-call | tf_op jit(solution)/shard_map/layer/pallas_call | solution.py:337
  72.5 1.3 %copy.13 = bf16[4,1792]{1,0:T(4,128)(2,1)} copy(bf16[4,1792]{1,0:T(4,128)(2,1)} %layer.1) | data formatting | bytes 28672
where the time goes:
time: 74.1 us; the launch traced here: 73.9 us
  Pallas kernels  71.2 us (96%)
  local copies, waits for them, and re-layouts  2.61 us (4%)
    pallas_call x1, Pallas kernels, per_device(): pl.pallas_call(functools.partial(layer_kernel, n, n_role, n_seq), out_sha...  71.2 us

commit v1 on v0

--- a/solution.py
+++ b/solution.py
@@ -309,7 +309,7 @@
     return depth
 
 
-def per_device(sizes, queries, cache, lengths, positions, value_up_weight, out_proj, residual,
+def per_device_latents(sizes, queries, cache, lengths, positions, value_up_weight, out_proj, residual,
                norm_gain, gate_weight, up_weight, down_weight):
     n, n_role, n_seq = sizes
     nr = n_role * n_seq
@@ -386,6 +386,427 @@
       residual, norm_gain.reshape(1, dd), *ws)
 
 
+LOG2E = 1.4426950408889634
+
+
+def by_distance(n, me):
+    found = []
+    for i in range(n - 1):
+        k = jnp.int32(0)
+        for z in range(n):
+            others = sorted((j for j in range(n) if j != z), key=lambda j: (abs(j - z), j))
+            k = jnp.where(me == z, others[i], k)
+        found.append(k)
+    return found
+
+
+def cut(width):
+    unit = 256 if width % 256 == 0 else 128
+    if width % unit or width < 2 * unit:
+        return [(0, width)]
+    first = -(-(width // unit) // 2) * unit
+    return [(0, first), (first, width)]
+
+
+def heads_kernel(n, n_role, n_seq, q_hbm, cache_hbm, len_ref, pos_ref, vu_hbm, res_hbm, gain_hbm,
+                 wo_hbm, wg_hbm, wu_hbm, wd_hbm, out_ref,
+                 q_ref, cache, vu, res_ref, gain_ref, wo, wg, wu, wd,
+                 qn_send, qr_send, qn_all, qr_all, o_send, o_recv, st_send, st_recv, w_ref,
+                 a_head, v_send, xv, acc, po_send, po_recv, resid, ss_send, ss_recv,
+                 g_acc, u_acc, gu_send, gu_recv, h_send, h_all, h_full, dn, dn_send, dn_recv,
+                 lsem, wsem, qsem, vusem, osem, ssem, vsem, posem, sssem, gusem, hsem, dnsem):
+    nr = n_role * n_seq
+    me = lax.axis_index("ctx")
+    role, seq = lax.axis_index("role"), lax.axis_index("seq")
+    fme = role * n_seq + seq
+    near = by_distance(n, me)
+    mates = []
+    for dr in range(n_role):
+        for ds in range(n_seq):
+            if dr or ds:
+                r, s = lax.rem(role + dr, n_role), lax.rem(seq + ds, n_seq)
+                mates.append((r * n_seq + s, {"role": r, "seq": s}))
+    seqs, span, width = q_ref.shape
+    context = cache.shape[2]
+    heads = span // MTP
+    hk = heads // nr
+    rope = width - LATENT
+    lat = LATENT // nr
+    own = n - 1
+
+    q_copy = pltpu.make_async_copy(q_hbm, q_ref, lsem.at[0])
+    q_copy.start()
+    cache_copies = [
+        pltpu.make_async_copy(cache_hbm, cache.at[:, pl.ds(0, width), :], lsem.at[1]),
+        pltpu.make_async_copy(cache_hbm.at[:, pl.ds(LATENT, rope), :],
+                              cache.at[:, pl.ds(width, rope), :], lsem.at[2]),
+    ]
+    for c in cache_copies:
+        c.start()
+    barrier = pltpu.get_barrier_semaphore()
+    for k in near:
+        pl.semaphore_signal(barrier, inc=1, device_id={"ctx": k}, device_id_type=MESH)
+    for _, device in mates:
+        pl.semaphore_signal(barrier, inc=1, device_id=device, device_id_type=MESH)
+    vu_own = pltpu.make_async_copy(
+        vu_hbm.at[pl.ds(pl.multiple_of(fme * hk, hk), hk)],
+        vu.at[:, pl.ds(pl.multiple_of(fme * lat, lat), lat), :], lsem.at[3])
+    vu_own.start()
+    res_copy = pltpu.make_async_copy(res_hbm, res_ref, lsem.at[4])
+    res_copy.start()
+    gain_copy = pltpu.make_async_copy(gain_hbm, gain_ref.at[0], lsem.at[5])
+    gain_copy.start()
+
+    q_copy.wait()
+    for s in range(seqs):
+        qn, qr = [], []
+        for k in range(nr):
+            for t in range(MTP):
+                at = t * heads + k * hk
+                rows = q_ref[s, at:at + hk, :].astype(f32)
+                qn.append(rows[:, :LATENT])
+                qr.append(rows[:, LATENT:])
+        qn_send[s] = jnp.concatenate(qn, axis=0).astype(bf16)
+        qr = jnp.concatenate(qr, axis=0)
+        qr_send[s] = jnp.concatenate([qr[:span // 2], qr[span // 2:]], axis=1).astype(bf16)
+    weights = []
+    for which, (hbm, vmem) in enumerate(((wo_hbm, wo), (wg_hbm, wg), (wu_hbm, wu), (wd_hbm, wd))):
+        weights.append(pltpu.make_async_copy(hbm, vmem, wsem.at[which]))
+    for c in weights:
+        c.start()
+    pl.semaphore_wait(barrier, len(near) + len(mates))
+
+    sent = []
+
+    def send(src, dst, send_sem, recv_sem, device):
+        c = remote(src, dst, send_sem, recv_sem, device)
+        c.start()
+        sent.append(c)
+
+    def drain():
+        for c in sent:
+            c.wait_send()
+        sent.clear()
+
+    for s in range(seqs):
+        for k in near[::-1]:
+            send(qn_send.at[s], qn_all.at[me, s], qsem.at[0, s, k], qsem.at[1, s, me], {"ctx": k})
+            send(qr_send.at[s], qr_all.at[me, s], qsem.at[2, s, k], qsem.at[3, s, me], {"ctx": k})
+    for k, device in mates:
+        send(vu_hbm.at[pl.ds(pl.multiple_of(k * hk, hk), hk)],
+             vu.at[:, pl.ds(pl.multiple_of(fme * lat, lat), lat), :],
+             vusem.at[0, k], vusem.at[1, fme], device)
+
+    column = lax.broadcasted_iota(jnp.int32, (span, context), 1)
+    row = lax.broadcasted_iota(jnp.int32, (span, 1), 0)
+    even = lax.rem(row, MTP * hk) < hk
+    lane = lax.broadcasted_iota(jnp.int32, (span, 128), 1)
+    half = lax.broadcasted_iota(jnp.int32, (span // 2, 2 * rope), 1) < rope
+    ends = []
+    for s in range(seqs):
+        limit = jnp.where(even, pos_ref[MTP * s], pos_ref[MTP * s + 1]) + 1
+        ends.append(jnp.minimum(limit, len_ref[s]) - me * context)
+
+    def block(qn, qr, s, slot):
+        zero = jnp.zeros_like(qr)
+        q = jnp.concatenate(
+            [qn, jnp.concatenate([jnp.where(half, qr, zero), jnp.where(half, zero, qr)], axis=0)],
+            axis=1)
+        keys = cache[s]
+        scores = jnp.dot(q, keys, preferred_element_type=f32) * (softmax_scale * LOG2E)
+        scores = jnp.where(column < ends[s], scores, -1e30)
+        top = jnp.maximum(jnp.max(scores, axis=1, keepdims=True), -1e29)
+        probs = jnp.exp2(scores - top).astype(bf16)
+        total = jnp.sum(probs.astype(f32), axis=1, keepdims=True)
+        out = lax.dot_general(
+            probs, keys[:LATENT], (((1,), (1,)), ((), ())), preferred_element_type=f32)
+        out = out.astype(bf16)
+        for k in range(nr):
+            o_send[slot, s, k] = out[k * MTP * hk:(k + 1) * MTP * hk]
+        st_send[slot, s] = jnp.where(lane == 0, top, total).T[0:2]
+
+    mine = me * nr + fme
+    for c in cache_copies:
+        c.wait()
+    home = []
+    for s in range(seqs):
+        block(qn_send[s], qr_send[s], s, own)
+        for k, device in mates:
+            send(o_send.at[own, s, k], o_recv.at[mine, s], osem.at[0, s, own, k],
+                 osem.at[1, s, me, fme], device)
+            send(st_send.at[own, s], st_recv.at[mine, s], ssem.at[0, s, own, k],
+                 ssem.at[1, s, me, fme], device)
+        for c in (
+            pltpu.make_async_copy(o_send.at[own, s, fme], o_recv.at[mine, s], osem.at[1, s, me, fme]),
+            pltpu.make_async_copy(st_send.at[own, s], st_recv.at[mine, s], ssem.at[1, s, me, fme]),
+        ):
+            c.start()
+    for s in range(seqs):
+        for i, b in enumerate(near):
+            there = {"ctx": b}
+            remote(qn_send.at[s], qn_all.at[b, s], qsem.at[0, s, b], qsem.at[1, s, b],
+                   there).wait_recv()
+            remote(qr_send.at[s], qr_all.at[b, s], qsem.at[2, s, b], qsem.at[3, s, b],
+                   there).wait_recv()
+            block(qn_all[b, s], qr_all[b, s], s, i)
+            for k in range(nr):
+                device = {"ctx": b, "role": k // n_seq, "seq": k % n_seq}
+                send(o_send.at[i, s, k], o_recv.at[mine, s], osem.at[0, s, i, k],
+                     osem.at[1, s, me, fme], device)
+                send(st_send.at[i, s], st_recv.at[mine, s], ssem.at[0, s, i, k],
+                     ssem.at[1, s, me, fme], device)
+
+    rows = seqs * MTP
+    all_rows = nr * rows
+    mine_at = pl.ds(pl.multiple_of(fme * MTP * hk, MTP * hk), MTP * hk)
+    first = {"ctx": near[0]}
+    for s in range(seqs):
+        tops, totals = [], []
+        for b in range(n):
+            for j in range(nr):
+                remote(st_send.at[0, s], st_recv.at[b * nr + j, s], ssem.at[0, s, 0, 0],
+                       ssem.at[1, s, b, j], first).wait_recv()
+            stats = [st_recv[b * nr + j, s] for j in range(nr)]
+            tops.append(jnp.concatenate([x[0:1] for x in stats], axis=0))
+            totals.append(jnp.concatenate([x[1:2] for x in stats], axis=0))
+        highest = functools.reduce(jnp.maximum, tops)
+        factors = [jnp.exp2(t - highest) for t in tops]
+        denom = sum(f * t for f, t in zip(factors, totals))
+        shares = jnp.concatenate([f / denom for f in factors], axis=0)
+        copies = -(-128 // (n * nr))
+        shares = jnp.concatenate([shares] * copies, axis=0)[:128]
+        w_ref[s] = shares.T
+        share = w_ref[s, mine_at, :]
+        for j in range(nr):
+            mixed = None
+            for b in range(n):
+                i = b * nr + j
+                remote(o_send.at[0, s, 0], o_recv.at[i, s], osem.at[0, s, 0, 0],
+                       osem.at[1, s, b, j], first).wait_recv()
+                term = share[:, i:i + 1] * o_recv[i, s].astype(f32)
+                mixed = term if mixed is None else mixed + term
+            for t in range(MTP):
+                a_head[:, j * rows + s * MTP + t, :] = mixed[t * hk:(t + 1) * hk]
+
+    vu_own.wait()
+    for k, device in mates:
+        remote(vu_hbm.at[pl.ds(0, hk)], vu.at[:, pl.ds(pl.multiple_of(k * lat, lat), lat), :],
+               vusem.at[0, k], vusem.at[1, k], device).wait_recv()
+    vdim = vu.shape[2]
+    for h in range(hk):
+        v_send[:, h * vdim:(h + 1) * vdim] = jnp.dot(
+            a_head[h].astype(bf16), vu[h], preferred_element_type=f32).astype(bf16)
+    for k, device in mates:
+        send(v_send, xv.at[fme], vsem.at[0, k], vsem.at[1, fme], device)
+    weights[0].wait()
+    deep = hk * vdim
+
+    def wo_rows(k):
+        return pl.ds(pl.multiple_of(k * deep, deep), deep)
+
+    acc[...] = jnp.dot(v_send[...], wo[wo_rows(fme), :], preferred_element_type=f32)
+
+    def arrived(k, device):
+        remote(v_send, xv.at[k], vsem.at[0, k], vsem.at[1, k], device).wait_recv()
+
+    early, late = mates[:n_seq - 1], mates[n_seq - 1:]
+    for k, device in early:
+        arrived(k, device)
+        acc[...] += jnp.dot(xv[k], wo[wo_rows(k), :], preferred_element_type=f32)
+    for k, device in late:
+        arrived(k, device)
+    dd = acc.shape[1]
+    parts = cut(dd)
+    for p, (c0, c1) in enumerate(parts):
+        total = acc[:, c0:c1]
+        for k, device in late:
+            total = total + jnp.dot(xv[k], wo[wo_rows(k), c0:c1], preferred_element_type=f32)
+        acc[:, c0:c1] = total
+        po_send[:, c0:c1] = total.astype(bf16)
+        for k in near[::-1]:
+            send(po_send.at[:, c0:c1], po_recv.at[me, :, c0:c1], posem.at[0, p, k],
+                 posem.at[1, p, me], {"ctx": k})
+    drain()
+    res_copy.wait()
+    gain_copy.wait()
+    weights[1].wait()
+    weights[2].wait()
+
+    part, crows = all_rows // nr, all_rows // n
+    ff = g_acc.shape[1]
+    fparts = [(f, min(f + 768, ff)) for f in range(0, ff, 768)]
+    sumsq = jnp.zeros((all_rows, 1), f32)
+    for p, (c0, c1) in enumerate(parts):
+        total = res_ref[:, c0:c1].astype(f32) + acc[:, c0:c1]
+        for k in near:
+            remote(po_send.at[:, c0:c1], po_recv.at[k, :, c0:c1], posem.at[0, p, k],
+                   posem.at[1, p, k], {"ctx": k}).wait_recv()
+            total = total + po_recv[k, :, c0:c1].astype(f32)
+        for k in range(n):
+            resid[k, :, c0:c1] = total[k * crows:(k + 1) * crows]
+        sumsq = sumsq + jnp.sum(total * total, axis=1, keepdims=True)
+        x = (total * gain_ref[:, c0:c1]).astype(bf16)
+        last = p == len(parts) - 1
+        if last:
+            wide = jnp.broadcast_to(sumsq, (all_rows, 128))
+            for k in range(nr):
+                ss_send[k] = wide[k * part:(k + 1) * part]
+            for k, device in mates:
+                send(ss_send.at[k], ss_recv.at[fme], sssem.at[0, k], sssem.at[1, fme], device)
+        for q, (f0, f1) in enumerate(fparts if last else [(0, ff)]):
+            for j, (w, a) in enumerate(((wg, g_acc), (wu, u_acc))):
+                y = jnp.dot(x, w[c0:c1, f0:f1], preferred_element_type=f32)
+                if p:
+                    y = y + a[:, f0:f1]
+                if not last:
+                    a[:, f0:f1] = y
+                    continue
+                for k in range(nr):
+                    gu_send[k, j, :, f0:f1] = y[k * part:(k + 1) * part].astype(bf16)
+            if last:
+                for k, device in mates:
+                    send(gu_send.at[k, :, :, f0:f1], gu_recv.at[fme, :, :, f0:f1],
+                         gusem.at[0, q, k], gusem.at[1, q, fme], device)
+    ss = ss_send[fme]
+    for k, device in mates:
+        remote(ss_send.at[k], ss_recv.at[k], sssem.at[0, k], sssem.at[1, k], device).wait_recv()
+        ss = ss + ss_recv[k]
+    inv = lax.rsqrt(ss[:, 0:1] / D + epsilon)
+    for q, (f0, f1) in enumerate(fparts):
+        gate = gu_send[fme, 0, :, f0:f1].astype(f32)
+        up = gu_send[fme, 1, :, f0:f1].astype(f32)
+        for k, device in mates:
+            remote(gu_send.at[k, :, :, f0:f1], gu_recv.at[k, :, :, f0:f1], gusem.at[0, q, k],
+                   gusem.at[1, q, k], device).wait_recv()
+            gate = gate + gu_recv[k, 0, :, f0:f1].astype(f32)
+            up = up + gu_recv[k, 1, :, f0:f1].astype(f32)
+        gate = gate * inv
+        up = up * inv
+        h = (gate / (1.0 + jnp.exp(-gate)) * up).astype(bf16)
+        h_send[:, f0:f1] = h
+        h_all[fme, :, f0:f1] = h
+        for k, device in mates:
+            send(h_send.at[:, f0:f1], h_all.at[fme, :, f0:f1], hsem.at[0, q, k],
+                 hsem.at[1, q, fme], device)
+    weights[3].wait()
+    for q, (f0, f1) in enumerate(fparts):
+        for k, device in mates:
+            remote(h_send.at[:, f0:f1], h_all.at[k, :, f0:f1], hsem.at[0, q, k],
+                   hsem.at[1, q, k], device).wait_recv()
+        for k in range(nr):
+            h_full[k * part:(k + 1) * part, f0:f1] = h_all[k, :, f0:f1].astype(f32)
+        x = h_full[:, f0:f1].astype(bf16)
+        last = q == len(fparts) - 1
+        for p, (c0, c1) in enumerate(parts if last else [(0, dd)]):
+            y = jnp.dot(x, wd[f0:f1, c0:c1], preferred_element_type=f32)
+            if q:
+                y = y + acc[:, c0:c1]
+            if not last:
+                acc[:, c0:c1] = y
+                continue
+            for k in range(n):
+                piece = y[k * crows:(k + 1) * crows]
+                dn[k, :, c0:c1] = piece
+                dn_send[k, :, c0:c1] = piece.astype(bf16)
+            for k in near[::-1]:
+                send(dn_send.at[k, :, c0:c1], dn_recv.at[me, :, c0:c1], dnsem.at[0, p, k],
+                     dnsem.at[1, p, me], {"ctx": k})
+    drain()
+    for p, (c0, c1) in enumerate(parts):
+        result = resid[me, :, c0:c1] + dn[me, :, c0:c1]
+        for k in near:
+            remote(dn_send.at[k, :, c0:c1], dn_recv.at[k, :, c0:c1], dnsem.at[0, p, k],
+                   dnsem.at[1, p, k], {"ctx": k}).wait_recv()
+            result = result + dn_recv[k, :, c0:c1].astype(f32)
+        out_ref[:, c0:c1] = result.astype(bf16)
+
+
+def per_device(sizes, queries, cache, lengths, positions, value_up_weight, out_proj, residual,
+               norm_gain, gate_weight, up_weight, down_weight):
+    n, n_role, n_seq = sizes
+    nr = n_role * n_seq
+    rows, heads, width = queries.shape
+    seqs, context = cache.shape[:2]
+    rope = width - LATENT
+    if heads % (8 * nr) or 2 * rope != 128 or n < 2 or nr < 2:
+        return per_device_latents(
+            sizes, queries, cache, lengths, positions, value_up_weight, out_proj, residual,
+            norm_gain, gate_weight, up_weight, down_weight)
+    hk = heads // nr
+    span = rows * heads // seqs
+    vdim = value_up_weight.shape[2]
+    all_rows, dd = residual.shape
+    ff = gate_weight.shape[1]
+    part, crows = all_rows // nr, all_rows // n
+    nf = -(-ff // 768)
+    vmem = pl.BlockSpec(memory_space=pltpu.VMEM)
+    smem = pl.BlockSpec(memory_space=pltpu.SMEM)
+    hbm = pl.BlockSpec(memory_space=pl.ANY)
+    V = pltpu.VMEM
+    sems = lambda *k: pltpu.SemaphoreType.DMA(k)
+    return pl.pallas_call(
+        functools.partial(heads_kernel, n, n_role, n_seq),
+        out_shape=jax.ShapeDtypeStruct((crows, dd), bf16),
+        in_specs=[hbm, hbm, smem, smem] + [hbm] * 7,
+        out_specs=vmem,
+        scratch_shapes=[
+            V((seqs, span, width), bf16),
+            V((seqs, width + rope, context), bf16),
+            V((hk, LATENT, vdim), bf16),
+            V((all_rows, dd), bf16),
+            V((1, dd), f32),
+            V(out_proj.shape, bf16),
+            V(gate_weight.shape, bf16),
+            V(up_weight.shape, bf16),
+            V(down_weight.shape, bf16),
+            V((seqs, span, LATENT), bf16),
+            V((seqs, span // 2, 2 * rope), bf16),
+            V((n, seqs, span, LATENT), bf16),
+            V((n, seqs, span // 2, 2 * rope), bf16),
+            V((n, seqs, nr, MTP * hk, LATENT), bf16),
+            V((n * nr, seqs, MTP * hk, LATENT), bf16),
+            V((n, seqs, 2, span), f32),
+            V((n * nr, seqs, 2, span), f32),
+            V((seqs, span, 128), f32),
+            V((hk, all_rows, LATENT), f32),
+            V((all_rows, hk * vdim), bf16),
+            V((nr, all_rows, hk * vdim), bf16),
+            V((all_rows, dd), f32),
+            V((all_rows, dd), bf16),
+            V((n, all_rows, dd), bf16),
+            V((n, crows, dd), f32),
+            V((nr, part, 128), f32),
+            V((nr, part, 128), f32),
+            V((all_rows, ff), f32),
+            V((all_rows, ff), f32),
+            V((nr, 2, part, ff), bf16),
+            V((nr, 2, part, ff), bf16),
+            V((part, ff), bf16),
+            V((nr, part, ff), bf16),
+            V((all_rows, ff), f32),
+            V((n, crows, dd), f32),
+            V((n, crows, dd), bf16),
+            V((n, crows, dd), bf16),
+            sems(6),
+            sems(4),
+            sems(4, seqs, n),
+            sems(2, nr),
+            sems(2, seqs, n, nr),
+            sems(2, seqs, n, nr),
+            sems(2, nr),
+            sems(2, 2, n),
+            sems(2, nr),
+            sems(2, nf, nr),
+            sems(2, nf, nr),
+            sems(2, 2, n),
+        ],
+        compiler_params=pltpu.CompilerParams(
+            collective_id=0, has_side_effects=True, vmem_limit_bytes=VMEM_BYTES),
+        name="layer",
+    )(queries.reshape(seqs, span, width), cache.transpose(0, 2, 1), lengths, positions, value_up_weight,
+      residual, norm_gain, out_proj, gate_weight, up_weight, down_weight)
+
+
 def solution(mesh):
     placed = (
         P(("groups", "role", "seq"), "ctx", None),

time: 74.1 us -> 60.6 us (0.82)
  Pallas kernels: 71.2 us -> 59 us
  local copies, waits for them, and re-layouts: 2.61 us -> 1.32 us
    pallas_call x1, Pallas kernels: 71.2 us -> 59 us  [per_device(): pl.pallas_call(functools.partial(heads_kernel, n, n_role, n_seq), out_sha...]
    reshape x1 -> x0, local copies, waits for them, and re-layouts: 1.29 us -> none  [per_device(): norm_gain.reshape(1, dd)]
where the time goes in v1:
time: 60.6 us; the launch traced here: 60.3 us
  Pallas kernels  59 us (97%)
  local copies, waits for them, and re-layouts  1.32 us (2%)
    pallas_call x1, Pallas kernels, per_device(): pl.pallas_call(functools.partial(heads_kernel, n, n_role, n_seq), out_sha...  59 us
    unnamed x1, local copies, waits for them, and re-layouts  1.32 us

profile of v1, /device:TPU:0, one launch (start us, length us, event | category | flops | bytes accessed | tf_op | source)
XLA Modules:
  0.0 60.3 jit_solution(14759667064294274680)
XLA Ops:
  0.0 59.0 %layer.1 = bf16[4,1792]{1,0:T(4,128)(2,1)} custom-call(bf16[2,64,576]{2,1,0:T(8,128)(2,1)} %bitcast.3, bf16[2,576,1024]{2,1,0:T(8,128)(2,1)} %bitcast.2, s32[2]{0:T(128)} %len_ref.1, s32[4]{0:T(128)} %pos_ref.1, bf16[32,128,128]{2,1,0:T(8,128)(2,1)} %vu_hbm.1, bf16[16,1792]{1,0:T(8,128)(2,1)} %res_hbm.1, f32[1792]{0:T(1024)} %gain_hbm.1, ...), custom_call_target="tpu_custom_call" | custom-call | tf_op jit(solution)/shard_map/layer/pallas_call | solution.py:747
  59.0 1.3 %copy.13 = bf16[4,1792]{1,0:T(4,128)(2,1)} copy(bf16[4,1792]{1,0:T(4,128)(2,1)} %layer.1) | data formatting | bytes 28672

commit v2 on v1

--- a/solution.py
+++ b/solution.py
@@ -483,15 +483,49 @@
         c.start()
         sent.append(c)
 
+    passed = []
+
     def drain():
         for c in sent:
             c.wait_send()
         sent.clear()
-
+        if passed:
+            @pl.when(inner == 1)
+            def _():
+                for b, s in passed:
+                    for r, ref in ((0, qn_send), (2, qr_send)):
+                        remote(ref.at[s], ref.at[s], qsem.at[r, s, b, beside],
+                               qsem.at[r + 1, s, b, 0], {"ctx": beside}).wait_send()
+            passed.clear()
+
+    def pass_on(b, s, k, source):
+        qn, qr = (qn_send.at[s], qr_send.at[s]) if source is None else (qn_all.at[b, s], qr_all.at[b, s])
+        given = [
+            remote(qn, qn_all.at[b, s], qsem.at[0, s, b, k], qsem.at[1, s, b, 0], {"ctx": k}),
+            remote(qr, qr_all.at[b, s], qsem.at[2, s, b, k], qsem.at[3, s, b, 0], {"ctx": k}),
+        ]
+        for c in given:
+            c.start()
+        return given
+
+    def take(b, s):
+        remote(qn_send.at[s], qn_all.at[b, s], qsem.at[0, s, b, b], qsem.at[1, s, b, 0],
+               {"ctx": b}).wait_recv()
+        remote(qr_send.at[s], qr_all.at[b, s], qsem.at[2, s, b, b], qsem.at[3, s, b, 0],
+               {"ctx": b}).wait_recv()
+
+    paired = n == 4
+    if paired:
+        beside = me + 1 - 2 * lax.rem(me, 2)
+        across = 2 - me // 2
+        beyond = 3 - 3 * (me // 2)
+        inner = lax.rem((me + 1) // 2, 2)
+        reach = [beside, across]
+    else:
+        reach = near[::-1]
     for s in range(seqs):
-        for k in near[::-1]:
-            send(qn_send.at[s], qn_all.at[me, s], qsem.at[0, s, k], qsem.at[1, s, me], {"ctx": k})
-            send(qr_send.at[s], qr_all.at[me, s], qsem.at[2, s, k], qsem.at[3, s, me], {"ctx": k})
+        for k in reach:
+            sent.extend(pass_on(me, s, k, None))
     for k, device in mates:
         send(vu_hbm.at[pl.ds(pl.multiple_of(k * hk, hk), hk)],
              vu.at[:, pl.ds(pl.multiple_of(fme * lat, lat), lat), :],
@@ -523,7 +557,8 @@
         out = out.astype(bf16)
         for k in range(nr):
             o_send[slot, s, k] = out[k * MTP * hk:(k + 1) * MTP * hk]
-        st_send[slot, s] = jnp.where(lane == 0, top, total).T[0:2]
+        stats = jnp.where(lane == 0, top, total).T
+        st_send[slot, s] = jnp.concatenate([stats[0:1], stats[1:2]], axis=1)
 
     mine = me * nr + fme
     for c in cache_copies:
@@ -541,20 +576,49 @@
             pltpu.make_async_copy(st_send.at[own, s], st_recv.at[mine, s], ssem.at[1, s, me, fme]),
         ):
             c.start()
-    for s in range(seqs):
-        for i, b in enumerate(near):
-            there = {"ctx": b}
-            remote(qn_send.at[s], qn_all.at[b, s], qsem.at[0, s, b], qsem.at[1, s, b],
-                   there).wait_recv()
-            remote(qr_send.at[s], qr_all.at[b, s], qsem.at[2, s, b], qsem.at[3, s, b],
-                   there).wait_recv()
-            block(qn_all[b, s], qr_all[b, s], s, i)
-            for k in range(nr):
-                device = {"ctx": b, "role": k // n_seq, "seq": k % n_seq}
-                send(o_send.at[i, s, k], o_recv.at[mine, s], osem.at[0, s, i, k],
-                     osem.at[1, s, me, fme], device)
-                send(st_send.at[i, s], st_recv.at[mine, s], ssem.at[0, s, i, k],
-                     ssem.at[1, s, me, fme], device)
+
+    def answer(b, s, slot):
+        block(qn_all[b, s], qr_all[b, s], s, slot)
+        for k in range(nr):
+            device = {"ctx": b, "role": k // n_seq, "seq": k % n_seq}
+            send(o_send.at[slot, s, k], o_recv.at[mine, s], osem.at[0, s, slot, k],
+                 osem.at[1, s, me, fme], device)
+            send(st_send.at[slot, s], st_recv.at[mine, s], ssem.at[0, s, slot, k],
+                 ssem.at[1, s, me, fme], device)
+
+    if paired:
+        def relay(b, s):
+            @pl.when(inner == 1)
+            def _():
+                take(b, s)
+                pass_on(b, s, beside, b)
+
+            passed.append((b, s))
+
+        def take_outer(b, s):
+            @pl.when(inner == 0)
+            def _():
+                take(b, s)
+
+        relay(across, 0)
+        for s in range(seqs):
+            take(beside, s)
+            answer(beside, s, 0)
+            if s == 0:
+                relay(beyond, 0)
+            take_outer(across, s)
+            answer(across, s, 1)
+            if s + 1 < seqs:
+                relay(across, s + 1)
+            take_outer(beyond, s)
+            answer(beyond, s, 2)
+            if s + 1 < seqs:
+                relay(beyond, s + 1)
+    else:
+        for s in range(seqs):
+            for i, b in enumerate(near):
+                take(b, s)
+                answer(b, s, i)
 
     rows = seqs * MTP
     all_rows = nr * rows
@@ -567,8 +631,9 @@
                 remote(st_send.at[0, s], st_recv.at[b * nr + j, s], ssem.at[0, s, 0, 0],
                        ssem.at[1, s, b, j], first).wait_recv()
             stats = [st_recv[b * nr + j, s] for j in range(nr)]
-            tops.append(jnp.concatenate([x[0:1] for x in stats], axis=0))
-            totals.append(jnp.concatenate([x[1:2] for x in stats], axis=0))
+            stats = jnp.concatenate(stats, axis=0)
+            tops.append(stats[:, :span])
+            totals.append(stats[:, span:])
         highest = functools.reduce(jnp.maximum, tops)
         factors = [jnp.exp2(t - highest) for t in tops]
         denom = sum(f * t for f, t in zip(factors, totals))
@@ -765,8 +830,8 @@
             V((n, seqs, span // 2, 2 * rope), bf16),
             V((n, seqs, nr, MTP * hk, LATENT), bf16),
             V((n * nr, seqs, MTP * hk, LATENT), bf16),
-            V((n, seqs, 2, span), f32),
-            V((n * nr, seqs, 2, span), f32),
+            V((n, seqs, 1, 2 * span), f32),
+            V((n * nr, seqs, 1, 2 * span), f32),
             V((seqs, span, 128), f32),
             V((hk, all_rows, LATENT), f32),
             V((all_rows, hk * vdim), bf16),
@@ -789,7 +854,7 @@
             V((n, crows, dd), bf16),
             sems(6),
             sems(4),
-            sems(4, seqs, n),
+            sems(4, seqs, n, n),
             sems(2, nr),
             sems(2, seqs, n, nr),
             sems(2, seqs, n, nr),

time: 60.6 us -> 56.7 us (0.936)
  Pallas kernels: 59 us -> 55.1 us
    pallas_call x1, Pallas kernels: 59 us -> 55.1 us  [per_device(): pl.pallas_call(functools.partial(heads_kernel, n, n_role, n_seq), out_sha...]
where the time goes in v2:
time: 56.7 us; the launch traced here: 56.4 us
  Pallas kernels  55.1 us (97%)
  local copies, waits for them, and re-layouts  1.32 us (2%)
    pallas_call x1, Pallas kernels, per_device(): pl.pallas_call(functools.partial(heads_kernel, n, n_role, n_seq), out_sha...  55.1 us
    unnamed x1, local copies, waits for them, and re-layouts  1.32 us

profile of v2, /device:TPU:0, one launch (start us, length us, event | category | flops | bytes accessed | tf_op | source)
XLA Modules:
  0.0 56.4 jit_solution(10064708917587278144)
XLA Ops:
  0.0 55.1 %layer.1 = bf16[4,1792]{1,0:T(4,128)(2,1)} custom-call(bf16[2,64,576]{2,1,0:T(8,128)(2,1)} %bitcast.3, bf16[2,576,1024]{2,1,0:T(8,128)(2,1)} %bitcast.2, s32[2]{0:T(128)} %len_ref.1, s32[4]{0:T(128)} %pos_ref.1, bf16[32,128,128]{2,1,0:T(8,128)(2,1)} %vu_hbm.1, bf16[16,1792]{1,0:T(8,128)(2,1)} %res_hbm.1, f32[1792]{0:T(1024)} %gain_hbm.1, ...), custom_call_target="tpu_custom_call" | custom-call | tf_op jit(solution)/shard_map/layer/pallas_call | solution.py:812
  55.1 1.3 %copy.13 = bf16[4,1792]{1,0:T(4,128)(2,1)} copy(bf16[4,1792]{1,0:T(4,128)(2,1)} %layer.1) | data formatting | bytes 28672

commit v3 on v2

--- a/solution.py
+++ b/solution.py
@@ -411,10 +411,10 @@
 def heads_kernel(n, n_role, n_seq, q_hbm, cache_hbm, len_ref, pos_ref, vu_hbm, res_hbm, gain_hbm,
                  wo_hbm, wg_hbm, wu_hbm, wd_hbm, out_ref,
                  q_ref, cache, vu, res_ref, gain_ref, wo, wg, wu, wd,
-                 qn_send, qr_send, qn_all, qr_all, o_send, o_recv, st_send, st_recv, w_ref,
+                 q_send, q_all, o_send, o_recv, st_send, st_recv, w_ref,
                  a_head, v_send, xv, acc, po_send, po_recv, resid, ss_send, ss_recv,
                  g_acc, u_acc, gu_send, gu_recv, h_send, h_all, h_full, dn, dn_send, dn_recv,
-                 lsem, wsem, qsem, vusem, osem, ssem, vsem, posem, sssem, gusem, hsem, dnsem):
+                 lsem, wsem, qsem, gone, osem, stsem, vsem, posem, gusem, hsem, dnsem, onesem):
     nr = n_role * n_seq
     me = lax.axis_index("ctx")
     role, seq = lax.axis_index("role"), lax.axis_index("seq")
@@ -433,6 +433,7 @@
     rope = width - LATENT
     lat = LATENT // nr
     own = n - 1
+    extra = span * rope // LATENT
 
     q_copy = pltpu.make_async_copy(q_hbm, q_ref, lsem.at[0])
     q_copy.start()
@@ -466,9 +467,11 @@
                 rows = q_ref[s, at:at + hk, :].astype(f32)
                 qn.append(rows[:, :LATENT])
                 qr.append(rows[:, LATENT:])
-        qn_send[s] = jnp.concatenate(qn, axis=0).astype(bf16)
+        q_send[s, :span] = jnp.concatenate(qn, axis=0).astype(bf16)
         qr = jnp.concatenate(qr, axis=0)
-        qr_send[s] = jnp.concatenate([qr[:span // 2], qr[span // 2:]], axis=1).astype(bf16)
+        qr = jnp.concatenate([qr[:span // 2], qr[span // 2:]], axis=1)
+        q_send[s, span:] = jnp.concatenate(
+            [qr[i:i + extra] for i in range(0, span // 2, extra)], axis=1).astype(bf16)
     weights = []
     for which, (hbm, vmem) in enumerate(((wo_hbm, wo), (wg_hbm, wg), (wu_hbm, wu), (wd_hbm, wd))):
         weights.append(pltpu.make_async_copy(hbm, vmem, wsem.at[which]))
@@ -476,43 +479,19 @@
         c.start()
     pl.semaphore_wait(barrier, len(near) + len(mates))
 
-    sent = []
-
-    def send(src, dst, send_sem, recv_sem, device):
-        c = remote(src, dst, send_sem, recv_sem, device)
-        c.start()
-        sent.append(c)
-
-    passed = []
-
-    def drain():
-        for c in sent:
-            c.wait_send()
-        sent.clear()
-        if passed:
-            @pl.when(inner == 1)
-            def _():
-                for b, s in passed:
-                    for r, ref in ((0, qn_send), (2, qr_send)):
-                        remote(ref.at[s], ref.at[s], qsem.at[r, s, b, beside],
-                               qsem.at[r + 1, s, b, 0], {"ctx": beside}).wait_send()
-            passed.clear()
-
-    def pass_on(b, s, k, source):
-        qn, qr = (qn_send.at[s], qr_send.at[s]) if source is None else (qn_all.at[b, s], qr_all.at[b, s])
-        given = [
-            remote(qn, qn_all.at[b, s], qsem.at[0, s, b, k], qsem.at[1, s, b, 0], {"ctx": k}),
-            remote(qr, qr_all.at[b, s], qsem.at[2, s, b, k], qsem.at[3, s, b, 0], {"ctx": k}),
-        ]
-        for c in given:
-            c.start()
-        return given
+    Q, RELAY, VU, O, ST, VAL, PO, SS, GU, H, DN = range(11)
+
+    def send(src, dst, kind, recv_sem, device):
+        remote(src, dst, gone.at[kind], recv_sem, device).start()
+
+    def all_gone(kind, like):
+        remote(like, like, gone.at[kind], gone.at[kind], {"ctx": near[0]}).wait_send()
+
+    def all_here(like, recv_sem):
+        remote(like, like, gone.at[0], recv_sem, {"ctx": near[0]}).wait_recv()
 
     def take(b, s):
-        remote(qn_send.at[s], qn_all.at[b, s], qsem.at[0, s, b, b], qsem.at[1, s, b, 0],
-               {"ctx": b}).wait_recv()
-        remote(qr_send.at[s], qr_all.at[b, s], qsem.at[2, s, b, b], qsem.at[3, s, b, 0],
-               {"ctx": b}).wait_recv()
+        all_here(q_all.at[b, s], qsem.at[s, b])
 
     paired = n == 4
     if paired:
@@ -525,11 +504,10 @@
         reach = near[::-1]
     for s in range(seqs):
         for k in reach:
-            sent.extend(pass_on(me, s, k, None))
+            send(q_send.at[s], q_all.at[me, s], Q, qsem.at[s, me], {"ctx": k})
     for k, device in mates:
         send(vu_hbm.at[pl.ds(pl.multiple_of(k * hk, hk), hk)],
-             vu.at[:, pl.ds(pl.multiple_of(fme * lat, lat), lat), :],
-             vusem.at[0, k], vusem.at[1, fme], device)
+             vu.at[:, pl.ds(pl.multiple_of(fme * lat, lat), lat), :], VU, onesem.at[0], device)
 
     column = lax.broadcasted_iota(jnp.int32, (span, context), 1)
     row = lax.broadcasted_iota(jnp.int32, (span, 1), 0)
@@ -541,10 +519,13 @@
         limit = jnp.where(even, pos_ref[MTP * s], pos_ref[MTP * s + 1]) + 1
         ends.append(jnp.minimum(limit, len_ref[s]) - me * context)
 
-    def block(qn, qr, s, slot):
+    def block(queries, s, slot):
+        qn, qr = queries[:span], queries[span:].astype(f32)
+        qr = jnp.concatenate([qr[:, i:i + 128] for i in range(0, LATENT, 128)], axis=0)
         zero = jnp.zeros_like(qr)
         q = jnp.concatenate(
-            [qn, jnp.concatenate([jnp.where(half, qr, zero), jnp.where(half, zero, qr)], axis=0)],
+            [qn, jnp.concatenate([jnp.where(half, qr, zero), jnp.where(half, zero, qr)],
+                                 axis=0).astype(bf16)],
             axis=1)
         keys = cache[s]
         scores = jnp.dot(q, keys, preferred_element_type=f32) * (softmax_scale * LOG2E)
@@ -563,37 +544,30 @@
     mine = me * nr + fme
     for c in cache_copies:
         c.wait()
-    home = []
     for s in range(seqs):
-        block(qn_send[s], qr_send[s], s, own)
+        block(q_send[s], s, own)
         for k, device in mates:
-            send(o_send.at[own, s, k], o_recv.at[mine, s], osem.at[0, s, own, k],
-                 osem.at[1, s, me, fme], device)
-            send(st_send.at[own, s], st_recv.at[mine, s], ssem.at[0, s, own, k],
-                 ssem.at[1, s, me, fme], device)
+            send(o_send.at[own, s, k], o_recv.at[mine, s], O, osem.at[s], device)
+            send(st_send.at[own, s], st_recv.at[mine, s], ST, stsem.at[s], device)
         for c in (
-            pltpu.make_async_copy(o_send.at[own, s, fme], o_recv.at[mine, s], osem.at[1, s, me, fme]),
-            pltpu.make_async_copy(st_send.at[own, s], st_recv.at[mine, s], ssem.at[1, s, me, fme]),
+            pltpu.make_async_copy(o_send.at[own, s, fme], o_recv.at[mine, s], osem.at[s]),
+            pltpu.make_async_copy(st_send.at[own, s], st_recv.at[mine, s], stsem.at[s]),
         ):
             c.start()
 
     def answer(b, s, slot):
-        block(qn_all[b, s], qr_all[b, s], s, slot)
+        block(q_all[b, s], s, slot)
         for k in range(nr):
             device = {"ctx": b, "role": k // n_seq, "seq": k % n_seq}
-            send(o_send.at[slot, s, k], o_recv.at[mine, s], osem.at[0, s, slot, k],
-                 osem.at[1, s, me, fme], device)
-            send(st_send.at[slot, s], st_recv.at[mine, s], ssem.at[0, s, slot, k],
-                 ssem.at[1, s, me, fme], device)
+            send(o_send.at[slot, s, k], o_recv.at[mine, s], O, osem.at[s], device)
+            send(st_send.at[slot, s], st_recv.at[mine, s], ST, stsem.at[s], device)
 
     if paired:
         def relay(b, s):
             @pl.when(inner == 1)
             def _():
                 take(b, s)
-                pass_on(b, s, beside, b)
-
-            passed.append((b, s))
+                send(q_all.at[b, s], q_all.at[b, s], RELAY, qsem.at[s, b], {"ctx": beside})
 
         def take_outer(b, s):
             @pl.when(inner == 0)
@@ -623,13 +597,10 @@
     rows = seqs * MTP
     all_rows = nr * rows
     mine_at = pl.ds(pl.multiple_of(fme * MTP * hk, MTP * hk), MTP * hk)
-    first = {"ctx": near[0]}
     for s in range(seqs):
+        all_here(st_recv.at[:, s], stsem.at[s])
         tops, totals = [], []
         for b in range(n):
-            for j in range(nr):
-                remote(st_send.at[0, s], st_recv.at[b * nr + j, s], ssem.at[0, s, 0, 0],
-                       ssem.at[1, s, b, j], first).wait_recv()
             stats = [st_recv[b * nr + j, s] for j in range(nr)]
             stats = jnp.concatenate(stats, axis=0)
             tops.append(stats[:, :span])
@@ -642,27 +613,25 @@
         shares = jnp.concatenate([shares] * copies, axis=0)[:128]
         w_ref[s] = shares.T
         share = w_ref[s, mine_at, :]
+        all_here(o_recv.at[:, s], osem.at[s])
         for j in range(nr):
             mixed = None
             for b in range(n):
                 i = b * nr + j
-                remote(o_send.at[0, s, 0], o_recv.at[i, s], osem.at[0, s, 0, 0],
-                       osem.at[1, s, b, j], first).wait_recv()
                 term = share[:, i:i + 1] * o_recv[i, s].astype(f32)
                 mixed = term if mixed is None else mixed + term
             for t in range(MTP):
                 a_head[:, j * rows + s * MTP + t, :] = mixed[t * hk:(t + 1) * hk]
 
     vu_own.wait()
-    for k, device in mates:
-        remote(vu_hbm.at[pl.ds(0, hk)], vu.at[:, pl.ds(pl.multiple_of(k * lat, lat), lat), :],
-               vusem.at[0, k], vusem.at[1, k], device).wait_recv()
+    others = len(mates)
+    all_here(vu.at[:, :others * lat], onesem.at[0])
     vdim = vu.shape[2]
     for h in range(hk):
         v_send[:, h * vdim:(h + 1) * vdim] = jnp.dot(
             a_head[h].astype(bf16), vu[h], preferred_element_type=f32).astype(bf16)
     for k, device in mates:
-        send(v_send, xv.at[fme], vsem.at[0, k], vsem.at[1, fme], device)
+        send(v_send, xv.at[fme], VAL, vsem.at[fme], device)
     weights[0].wait()
     deep = hk * vdim
 
@@ -672,7 +641,7 @@
     acc[...] = jnp.dot(v_send[...], wo[wo_rows(fme), :], preferred_element_type=f32)
 
     def arrived(k, device):
-        remote(v_send, xv.at[k], vsem.at[0, k], vsem.at[1, k], device).wait_recv()
+        all_here(xv.at[k], vsem.at[k])
 
     early, late = mates[:n_seq - 1], mates[n_seq - 1:]
     for k, device in early:
@@ -689,9 +658,16 @@
         acc[:, c0:c1] = total
         po_send[:, c0:c1] = total.astype(bf16)
         for k in near[::-1]:
-            send(po_send.at[:, c0:c1], po_recv.at[me, :, c0:c1], posem.at[0, p, k],
-                 posem.at[1, p, me], {"ctx": k})
-    drain()
+            send(po_send.at[:, c0:c1], po_recv.at[me, :, c0:c1], PO, posem.at[p], {"ctx": k})
+    all_gone(Q, q_all.at[:len(reach)])
+    if paired:
+        @pl.when(inner == 1)
+        def _():
+            all_gone(RELAY, q_all.at[:2])
+    all_gone(VU, vu.at[:, :others * lat])
+    all_gone(O, o_recv.at[:n * nr - 1])
+    all_gone(ST, st_recv.at[:n * nr - 1])
+    all_gone(VAL, xv.at[:others])
     res_copy.wait()
     gain_copy.wait()
     weights[1].wait()
@@ -703,9 +679,8 @@
     sumsq = jnp.zeros((all_rows, 1), f32)
     for p, (c0, c1) in enumerate(parts):
         total = res_ref[:, c0:c1].astype(f32) + acc[:, c0:c1]
+        all_here(po_recv.at[:n - 1, :, c0:c1], posem.at[p])
         for k in near:
-            remote(po_send.at[:, c0:c1], po_recv.at[k, :, c0:c1], posem.at[0, p, k],
-                   posem.at[1, p, k], {"ctx": k}).wait_recv()
             total = total + po_recv[k, :, c0:c1].astype(f32)
         for k in range(n):
             resid[k, :, c0:c1] = total[k * crows:(k + 1) * crows]
@@ -717,7 +692,7 @@
             for k in range(nr):
                 ss_send[k] = wide[k * part:(k + 1) * part]
             for k, device in mates:
-                send(ss_send.at[k], ss_recv.at[fme], sssem.at[0, k], sssem.at[1, fme], device)
+                send(ss_send.at[k], ss_recv.at[fme], SS, onesem.at[1], device)
         for q, (f0, f1) in enumerate(fparts if last else [(0, ff)]):
             for j, (w, a) in enumerate(((wg, g_acc), (wu, u_acc))):
                 y = jnp.dot(x, w[c0:c1, f0:f1], preferred_element_type=f32)
@@ -731,18 +706,17 @@
             if last:
                 for k, device in mates:
                     send(gu_send.at[k, :, :, f0:f1], gu_recv.at[fme, :, :, f0:f1],
-                         gusem.at[0, q, k], gusem.at[1, q, fme], device)
+                         GU, gusem.at[q], device)
     ss = ss_send[fme]
+    all_here(ss_recv.at[:others], onesem.at[1])
     for k, device in mates:
-        remote(ss_send.at[k], ss_recv.at[k], sssem.at[0, k], sssem.at[1, k], device).wait_recv()
         ss = ss + ss_recv[k]
     inv = lax.rsqrt(ss[:, 0:1] / D + epsilon)
     for q, (f0, f1) in enumerate(fparts):
         gate = gu_send[fme, 0, :, f0:f1].astype(f32)
         up = gu_send[fme, 1, :, f0:f1].astype(f32)
+        all_here(gu_recv.at[:others, :, :, f0:f1], gusem.at[q])
         for k, device in mates:
-            remote(gu_send.at[k, :, :, f0:f1], gu_recv.at[k, :, :, f0:f1], gusem.at[0, q, k],
-                   gusem.at[1, q, k], device).wait_recv()
             gate = gate + gu_recv[k, 0, :, f0:f1].astype(f32)
             up = up + gu_recv[k, 1, :, f0:f1].astype(f32)
         gate = gate * inv
@@ -751,13 +725,10 @@
         h_send[:, f0:f1] = h
         h_all[fme, :, f0:f1] = h
         for k, device in mates:
-            send(h_send.at[:, f0:f1], h_all.at[fme, :, f0:f1], hsem.at[0, q, k],
-                 hsem.at[1, q, fme], device)
+            send(h_send.at[:, f0:f1], h_all.at[fme, :, f0:f1], H, hsem.at[q], device)
     weights[3].wait()
     for q, (f0, f1) in enumerate(fparts):
-        for k, device in mates:
-            remote(h_send.at[:, f0:f1], h_all.at[k, :, f0:f1], hsem.at[0, q, k],
-                   hsem.at[1, q, k], device).wait_recv()
+        all_here(h_all.at[:others, :, f0:f1], hsem.at[q])
         for k in range(nr):
             h_full[k * part:(k + 1) * part, f0:f1] = h_all[k, :, f0:f1].astype(f32)
         x = h_full[:, f0:f1].astype(bf16)
@@ -774,16 +745,18 @@
                 dn[k, :, c0:c1] = piece
                 dn_send[k, :, c0:c1] = piece.astype(bf16)
             for k in near[::-1]:
-                send(dn_send.at[k, :, c0:c1], dn_recv.at[me, :, c0:c1], dnsem.at[0, p, k],
-                     dnsem.at[1, p, me], {"ctx": k})
-    drain()
+                send(dn_send.at[k, :, c0:c1], dn_recv.at[me, :, c0:c1], DN, dnsem.at[p], {"ctx": k})
+    all_gone(PO, po_recv.at[:n - 1])
+    all_gone(SS, ss_recv.at[:others])
+    all_gone(GU, gu_recv.at[:others])
+    all_gone(H, h_all.at[:others])
     for p, (c0, c1) in enumerate(parts):
         result = resid[me, :, c0:c1] + dn[me, :, c0:c1]
+        all_here(dn_recv.at[:n - 1, :, c0:c1], dnsem.at[p])
         for k in near:
-            remote(dn_send.at[k, :, c0:c1], dn_recv.at[k, :, c0:c1], dnsem.at[0, p, k],
-                   dnsem.at[1, p, k], {"ctx": k}).wait_recv()
             result = result + dn_recv[k, :, c0:c1].astype(f32)
         out_ref[:, c0:c1] = result.astype(bf16)
+    all_gone(DN, dn_recv.at[:n - 1])
 
 
 def per_device(sizes, queries, cache, lengths, positions, value_up_weight, out_proj, residual,
@@ -799,6 +772,7 @@
             norm_gain, gate_weight, up_weight, down_weight)
     hk = heads // nr
     span = rows * heads // seqs
+    extra = span * rope // LATENT
     vdim = value_up_weight.shape[2]
     all_rows, dd = residual.shape
     ff = gate_weight.shape[1]
@@ -824,10 +798,8 @@
             V(gate_weight.shape, bf16),
             V(up_weight.shape, bf16),
             V(down_weight.shape, bf16),
-            V((seqs, span, LATENT), bf16),
-            V((seqs, span // 2, 2 * rope), bf16),
-            V((n, seqs, span, LATENT), bf16),
-            V((n, seqs, span // 2, 2 * rope), bf16),
+            V((seqs, span + extra, LATENT), bf16),
+            V((n, seqs, span + extra, LATENT), bf16),
             V((n, seqs, nr, MTP * hk, LATENT), bf16),
             V((n * nr, seqs, MTP * hk, LATENT), bf16),
             V((n, seqs, 1, 2 * span), f32),
@@ -854,16 +826,16 @@
             V((n, crows, dd), bf16),
             sems(6),
             sems(4),
-            sems(4, seqs, n, n),
-            sems(2, nr),
-            sems(2, seqs, n, nr),
-            sems(2, seqs, n, nr),
-            sems(2, nr),
-            sems(2, 2, n),
-            sems(2, nr),
-            sems(2, nf, nr),
-            sems(2, nf, nr),
-            sems(2, 2, n),
+            sems(seqs, n),
+            sems(11),
+            sems(seqs),
+            sems(seqs),
+            sems(nr),
+            sems(2),
+            sems(nf),
+            sems(nf),
+            sems(2),
+            sems(2),
         ],
         compiler_params=pltpu.CompilerParams(
             collective_id=0, has_side_effects=True, vmem_limit_bytes=VMEM_BYTES),

time: 56.7 us -> 52.4 us (0.924)
  Pallas kernels: 55.1 us -> 50.8 us
    pallas_call x1, Pallas kernels: 55.1 us -> 50.8 us  [per_device(): pl.pallas_call(functools.partial(heads_kernel, n, n_role, n_seq), out_sha...]
where the time goes in v3:
time: 52.4 us; the launch traced here: 52.2 us
  Pallas kernels  50.8 us (97%)
  local copies, waits for them, and re-layouts  1.32 us (3%)
    pallas_call x1, Pallas kernels, per_device(): pl.pallas_call(functools.partial(heads_kernel, n, n_role, n_seq), out_sha...  50.8 us
    unnamed x1, local copies, waits for them, and re-layouts  1.32 us

profile of v3, /device:TPU:0, one launch (start us, length us, event | category | flops | bytes accessed | tf_op | source)
XLA Modules:
  0.0 52.2 jit_solution(1629361141588935778)
XLA Ops:
  0.0 50.8 %layer.1 = bf16[4,1792]{1,0:T(4,128)(2,1)} custom-call(bf16[2,64,576]{2,1,0:T(8,128)(2,1)} %bitcast.3, bf16[2,576,1024]{2,1,0:T(8,128)(2,1)} %bitcast.2, s32[2]{0:T(128)} %len_ref.1, s32[4]{0:T(128)} %pos_ref.1, bf16[32,128,128]{2,1,0:T(8,128)(2,1)} %vu_hbm.1, bf16[16,1792]{1,0:T(8,128)(2,1)} %res_hbm.1, f32[1792]{0:T(1024)} %gain_hbm.1, ...), custom_call_target="tpu_custom_call" | custom-call | tf_op jit(solution)/shard_map/layer/pallas_call | solution.py:786
  50.9 1.3 %copy.13 = bf16[4,1792]{1,0:T(4,128)(2,1)} copy(bf16[4,1792]{1,0:T(4,128)(2,1)} %layer.1) | data formatting | bytes 28672

commit v4 on v3

--- a/solution.py
+++ b/solution.py
@@ -412,7 +412,7 @@
                  wo_hbm, wg_hbm, wu_hbm, wd_hbm, out_ref,
                  q_ref, cache, vu, res_ref, gain_ref, wo, wg, wu, wd,
                  q_send, q_all, o_send, o_recv, st_send, st_recv, w_ref,
-                 a_head, v_send, xv, acc, po_send, po_recv, resid, ss_send, ss_recv,
+                 a_head, v_send, xv, acc, po, po_send, po_recv, resid, ss_send, ss_recv,
                  g_acc, u_acc, gu_send, gu_recv, h_send, h_all, h_full, dn, dn_send, dn_recv,
                  lsem, wsem, qsem, gone, osem, stsem, vsem, posem, gusem, hsem, dnsem, onesem):
     nr = n_role * n_seq
@@ -435,6 +435,16 @@
     own = n - 1
     extra = span * rope // LATENT
 
+    paired = n == 4
+    if paired:
+        beside = me + 1 - 2 * lax.rem(me, 2)
+        across = 2 - me // 2
+        beyond = 3 - 3 * (me // 2)
+        inner = lax.rem((me + 1) // 2, 2)
+        reach = [beside, across]
+    else:
+        reach = near[::-1]
+
     q_copy = pltpu.make_async_copy(q_hbm, q_ref, lsem.at[0])
     q_copy.start()
     cache_copies = [
@@ -445,8 +455,16 @@
     for c in cache_copies:
         c.start()
     barrier = pltpu.get_barrier_semaphore()
-    for k in near:
-        pl.semaphore_signal(barrier, inc=1, device_id={"ctx": k}, device_id_type=MESH)
+    if paired:
+        pl.semaphore_signal(barrier, inc=1, device_id={"ctx": beside}, device_id_type=MESH)
+
+        @pl.when(inner == 1)
+        def _():
+            for k in (across, beyond):
+                pl.semaphore_signal(barrier, inc=1, device_id={"ctx": k}, device_id_type=MESH)
+    else:
+        for k in near:
+            pl.semaphore_signal(barrier, inc=1, device_id={"ctx": k}, device_id_type=MESH)
     for _, device in mates:
         pl.semaphore_signal(barrier, inc=1, device_id=device, device_id_type=MESH)
     vu_own = pltpu.make_async_copy(
@@ -477,7 +495,7 @@
         weights.append(pltpu.make_async_copy(hbm, vmem, wsem.at[which]))
     for c in weights:
         c.start()
-    pl.semaphore_wait(barrier, len(near) + len(mates))
+    pl.semaphore_wait(barrier, len(reach) + len(mates))
 
     Q, RELAY, VU, O, ST, VAL, PO, SS, GU, H, DN = range(11)
 
@@ -493,15 +511,6 @@
     def take(b, s):
         all_here(q_all.at[b, s], qsem.at[s, b])
 
-    paired = n == 4
-    if paired:
-        beside = me + 1 - 2 * lax.rem(me, 2)
-        across = 2 - me // 2
-        beyond = 3 - 3 * (me // 2)
-        inner = lax.rem((me + 1) // 2, 2)
-        reach = [beside, across]
-    else:
-        reach = near[::-1]
     for s in range(seqs):
         for k in reach:
             send(q_send.at[s], q_all.at[me, s], Q, qsem.at[s, me], {"ctx": k})
@@ -597,12 +606,15 @@
     rows = seqs * MTP
     all_rows = nr * rows
     mine_at = pl.ds(pl.multiple_of(fme * MTP * hk, MTP * hk), MTP * hk)
-    for s in range(seqs):
+    vdim = vu.shape[2]
+    deep = hk * vdim
+    others = len(mates)
+
+    def merge(s):
         all_here(st_recv.at[:, s], stsem.at[s])
         tops, totals = [], []
         for b in range(n):
-            stats = [st_recv[b * nr + j, s] for j in range(nr)]
-            stats = jnp.concatenate(stats, axis=0)
+            stats = jnp.concatenate([st_recv[b * nr + j, s] for j in range(nr)], axis=0)
             tops.append(stats[:, :span])
             totals.append(stats[:, span:])
         highest = functools.reduce(jnp.maximum, tops)
@@ -621,44 +633,45 @@
                 term = share[:, i:i + 1] * o_recv[i, s].astype(f32)
                 mixed = term if mixed is None else mixed + term
             for t in range(MTP):
-                a_head[:, j * rows + s * MTP + t, :] = mixed[t * hk:(t + 1) * hk]
-
-    vu_own.wait()
-    others = len(mates)
-    all_here(vu.at[:, :others * lat], onesem.at[0])
-    vdim = vu.shape[2]
-    for h in range(hk):
-        v_send[:, h * vdim:(h + 1) * vdim] = jnp.dot(
-            a_head[h].astype(bf16), vu[h], preferred_element_type=f32).astype(bf16)
-    for k, device in mates:
-        send(v_send, xv.at[fme], VAL, vsem.at[fme], device)
-    weights[0].wait()
-    deep = hk * vdim
+                a_head[:, s, j * MTP + t, :] = mixed[t * hk:(t + 1) * hk]
+        if s == 0:
+            vu_own.wait()
+            all_here(vu.at[:, :others * lat], onesem.at[0])
+        for h in range(hk):
+            v_send[s, :, h * vdim:(h + 1) * vdim] = jnp.dot(
+                a_head[h, s].astype(bf16), vu[h], preferred_element_type=f32).astype(bf16)
+        for k, device in mates:
+            send(v_send.at[s], xv.at[s, fme], VAL, vsem.at[s, fme], device)
+
+    early, late = mates[:n_seq - 1], mates[n_seq - 1:]
+    dd = acc.shape[1]
+    parts = cut(dd)
 
     def wo_rows(k):
         return pl.ds(pl.multiple_of(k * deep, deep), deep)
 
-    acc[...] = jnp.dot(v_send[...], wo[wo_rows(fme), :], preferred_element_type=f32)
-
-    def arrived(k, device):
-        all_here(xv.at[k], vsem.at[k])
-
-    early, late = mates[:n_seq - 1], mates[n_seq - 1:]
-    for k, device in early:
-        arrived(k, device)
-        acc[...] += jnp.dot(xv[k], wo[wo_rows(k), :], preferred_element_type=f32)
-    for k, device in late:
-        arrived(k, device)
-    dd = acc.shape[1]
-    parts = cut(dd)
-    for p, (c0, c1) in enumerate(parts):
-        total = acc[:, c0:c1]
+    def project(s):
+        if s == 0:
+            weights[0].wait()
+        po[s] = jnp.dot(v_send[s], wo[wo_rows(fme), :], preferred_element_type=f32)
+        for k, device in early:
+            all_here(xv.at[s, k], vsem.at[s, k])
+            po[s] += jnp.dot(xv[s, k], wo[wo_rows(k), :], preferred_element_type=f32)
         for k, device in late:
-            total = total + jnp.dot(xv[k], wo[wo_rows(k), c0:c1], preferred_element_type=f32)
-        acc[:, c0:c1] = total
-        po_send[:, c0:c1] = total.astype(bf16)
-        for k in near[::-1]:
-            send(po_send.at[:, c0:c1], po_recv.at[me, :, c0:c1], PO, posem.at[p], {"ctx": k})
+            all_here(xv.at[s, k], vsem.at[s, k])
+        for p, (c0, c1) in enumerate(parts):
+            total = po[s, :, c0:c1]
+            for k, device in late:
+                total = total + jnp.dot(xv[s, k], wo[wo_rows(k), c0:c1], preferred_element_type=f32)
+            po[s, :, c0:c1] = total
+            po_send[s, :, c0:c1] = total.astype(bf16)
+            for k in near[::-1]:
+                send(po_send.at[s, :, c0:c1], po_recv.at[s, me, :, c0:c1], PO, posem.at[s, p],
+                     {"ctx": k})
+
+    for s in range(seqs):
+        merge(s)
+        project(s)
     all_gone(Q, q_all.at[:len(reach)])
     if paired:
         @pl.when(inner == 1)
@@ -667,7 +680,7 @@
     all_gone(VU, vu.at[:, :others * lat])
     all_gone(O, o_recv.at[:n * nr - 1])
     all_gone(ST, st_recv.at[:n * nr - 1])
-    all_gone(VAL, xv.at[:others])
+    all_gone(VAL, xv.at[:, :others])
     res_copy.wait()
     gain_copy.wait()
     weights[1].wait()
@@ -678,10 +691,15 @@
     fparts = [(f, min(f + 768, ff)) for f in range(0, ff, 768)]
     sumsq = jnp.zeros((all_rows, 1), f32)
     for p, (c0, c1) in enumerate(parts):
+        for s in range(seqs):
+            all_here(po_recv.at[s, :n - 1, :, c0:c1], posem.at[s, p])
+            total = po[s, :, c0:c1]
+            for k in near:
+                total = total + po_recv[s, k, :, c0:c1].astype(f32)
+            for j in range(nr):
+                at = j * rows + s * MTP
+                acc[at:at + MTP, c0:c1] = total[j * MTP:(j + 1) * MTP]
         total = res_ref[:, c0:c1].astype(f32) + acc[:, c0:c1]
-        all_here(po_recv.at[:n - 1, :, c0:c1], posem.at[p])
-        for k in near:
-            total = total + po_recv[k, :, c0:c1].astype(f32)
         for k in range(n):
             resid[k, :, c0:c1] = total[k * crows:(k + 1) * crows]
         sumsq = sumsq + jnp.sum(total * total, axis=1, keepdims=True)
@@ -746,7 +764,7 @@
                 dn_send[k, :, c0:c1] = piece.astype(bf16)
             for k in near[::-1]:
                 send(dn_send.at[k, :, c0:c1], dn_recv.at[me, :, c0:c1], DN, dnsem.at[p], {"ctx": k})
-    all_gone(PO, po_recv.at[:n - 1])
+    all_gone(PO, po_recv.at[:, :n - 1])
     all_gone(SS, ss_recv.at[:others])
     all_gone(GU, gu_recv.at[:others])
     all_gone(H, h_all.at[:others])
@@ -785,7 +803,7 @@
     sems = lambda *k: pltpu.SemaphoreType.DMA(k)
     return pl.pallas_call(
         functools.partial(heads_kernel, n, n_role, n_seq),
-        out_shape=jax.ShapeDtypeStruct((crows, dd), bf16),
+        out_shape=pltpu.VMEM((crows, dd), bf16),
         in_specs=[hbm, hbm, smem, smem] + [hbm] * 7,
         out_specs=vmem,
         scratch_shapes=[
@@ -805,12 +823,13 @@
             V((n, seqs, 1, 2 * span), f32),
             V((n * nr, seqs, 1, 2 * span), f32),
             V((seqs, span, 128), f32),
-            V((hk, all_rows, LATENT), f32),
-            V((all_rows, hk * vdim), bf16),
-            V((nr, all_rows, hk * vdim), bf16),
+            V((hk, seqs, all_rows // seqs, LATENT), f32),
+            V((seqs, all_rows // seqs, hk * vdim), bf16),
+            V((seqs, nr, all_rows // seqs, hk * vdim), bf16),
             V((all_rows, dd), f32),
-            V((all_rows, dd), bf16),
-            V((n, all_rows, dd), bf16),
+            V((seqs, all_rows // seqs, dd), f32),
+            V((seqs, all_rows // seqs, dd), bf16),
+            V((seqs, n, all_rows // seqs, dd), bf16),
             V((n, crows, dd), f32),
             V((nr, part, 128), f32),
             V((nr, part, 128), f32),
@@ -830,8 +849,8 @@
             sems(11),
             sems(seqs),
             sems(seqs),
-            sems(nr),
-            sems(2),
+            sems(seqs, nr),
+            sems(seqs, 2),
             sems(nf),
             sems(nf),
             sems(2),

time: 52.4 us -> 50.3 us (0.960)
  Pallas kernels: 50.8 us -> 49.5 us
  local copies, waits for them, and re-layouts: 1.32 us -> 0.6 us
    pallas_call x1, Pallas kernels: 50.8 us -> 49.5 us  [per_device(): pl.pallas_call(functools.partial(heads_kernel, n, n_role, n_seq), out_sha...]
    unnamed x1, local copies, waits for them, and re-layouts: 1.32 us -> 0.6 us
where the time goes in v4:
time: 50.3 us; the launch traced here: 50.1 us
  Pallas kernels  49.5 us (98%)
  local copies, waits for them, and re-layouts  0.6 us (1%)
    pallas_call x1, Pallas kernels, per_device(): pl.pallas_call(functools.partial(heads_kernel, n, n_role, n_seq), out_sha...  49.5 us

profile of v4, /device:TPU:0, one launch (start us, length us, event | category | flops | bytes accessed | tf_op | source)
XLA Modules:
  0.0 50.1 jit_solution(7916759271076217192)
XLA Ops:
  0.0 49.5 %layer.1 = bf16[4,1792]{1,0:T(4,128)(2,1)S(1)} custom-call(bf16[2,64,576]{2,1,0:T(8,128)(2,1)} %bitcast.3, bf16[2,576,1024]{2,1,0:T(8,128)(2,1)} %bitcast.2, s32[2]{0:T(128)} %len_ref.1, s32[4]{0:T(128)} %pos_ref.1, bf16[32,128,128]{2,1,0:T(8,128)(2,1)} %vu_hbm.1, bf16[16,1792]{1,0:T(8,128)(2,1)} %res_hbm.1, f32[1792]{0:T(1024)} %gain_hbm.1, ...), custom_call_target="tpu_custom_call" | custom-call | tf_op jit(solution)/shard_map/layer/pallas_call | solution.py:804
  49.5 0.6 %copy.13 = bf16[4,1792]{1,0:T(4,128)(2,1)} copy(bf16[4,1792]{1,0:T(4,128)(2,1)S(1)} %layer.1) | data formatting | bytes 28672

commit v5 on v4

--- a/solution.py
+++ b/solution.py
@@ -404,7 +404,7 @@
     unit = 256 if width % 256 == 0 else 128
     if width % unit or width < 2 * unit:
         return [(0, width)]
-    first = -(-(width // unit) // 2) * unit
+    first = width // unit // 2 * unit
     return [(0, first), (first, width)]
 
 
@@ -553,7 +553,7 @@
     mine = me * nr + fme
     for c in cache_copies:
         c.wait()
-    for s in range(seqs):
+    def home(s):
         block(q_send[s], s, own)
         for k, device in mates:
             send(o_send.at[own, s, k], o_recv.at[mine, s], O, osem.at[s], device)
@@ -583,22 +583,26 @@
             def _():
                 take(b, s)
 
+        home(0)
         relay(across, 0)
         for s in range(seqs):
             take(beside, s)
             answer(beside, s, 0)
             if s == 0:
                 relay(beyond, 0)
+            if s + 1 < seqs:
+                relay(across, s + 1)
             take_outer(across, s)
             answer(across, s, 1)
             if s + 1 < seqs:
-                relay(across, s + 1)
+                relay(beyond, s + 1)
             take_outer(beyond, s)
             answer(beyond, s, 2)
-            if s + 1 < seqs:
-                relay(beyond, s + 1)
+        for s in range(1, seqs):
+            home(s)
     else:
         for s in range(seqs):
+            home(s)
             for i, b in enumerate(near):
                 take(b, s)
                 answer(b, s, i)

time: 50.3 us -> 49.2 us (0.978)
  Pallas kernels: 49.5 us -> 48.5 us
    pallas_call x1, Pallas kernels: 49.5 us -> 48.5 us  [per_device(): pl.pallas_call(functools.partial(heads_kernel, n, n_role, n_seq), out_sha...]
where the time goes in v5:
time: 49.2 us; the launch traced here: 49.1 us
  Pallas kernels  48.5 us (99%)
  local copies, waits for them, and re-layouts  0.6 us (1%)
    pallas_call x1, Pallas kernels, per_device(): pl.pallas_call(functools.partial(heads_kernel, n, n_role, n_seq), out_sha...  48.5 us

profile of v5, /device:TPU:0, one launch (start us, length us, event | category | flops | bytes accessed | tf_op | source)
XLA Modules:
  0.0 49.1 jit_solution(1254939438394213077)
XLA Ops:
  0.0 48.5 %layer.1 = bf16[4,1792]{1,0:T(4,128)(2,1)S(1)} custom-call(bf16[2,64,576]{2,1,0:T(8,128)(2,1)} %bitcast.3, bf16[2,576,1024]{2,1,0:T(8,128)(2,1)} %bitcast.2, s32[2]{0:T(128)} %len_ref.1, s32[4]{0:T(128)} %pos_ref.1, bf16[32,128,128]{2,1,0:T(8,128)(2,1)} %vu_hbm.1, bf16[16,1792]{1,0:T(8,128)(2,1)} %res_hbm.1, f32[1792]{0:T(1024)} %gain_hbm.1, ...), custom_call_target="tpu_custom_call" | custom-call | tf_op jit(solution)/shard_map/layer/pallas_call | solution.py:808
  48.5 0.6 %copy.13 = bf16[4,1792]{1,0:T(4,128)(2,1)} copy(bf16[4,1792]{1,0:T(4,128)(2,1)S(1)} %layer.1) | data formatting | bytes 28672

commit v6 on v5

--- a/solution.py
+++ b/solution.py
@@ -654,13 +654,15 @@
     def wo_rows(k):
         return pl.ds(pl.multiple_of(k * deep, deep), deep)
 
-    def project(s):
+    def begin(s):
         if s == 0:
             weights[0].wait()
         po[s] = jnp.dot(v_send[s], wo[wo_rows(fme), :], preferred_element_type=f32)
         for k, device in early:
             all_here(xv.at[s, k], vsem.at[s, k])
             po[s] += jnp.dot(xv[s, k], wo[wo_rows(k), :], preferred_element_type=f32)
+
+    def finish(s):
         for k, device in late:
             all_here(xv.at[s, k], vsem.at[s, k])
         for p, (c0, c1) in enumerate(parts):
@@ -675,7 +677,10 @@
 
     for s in range(seqs):
         merge(s)
-        project(s)
+        if s:
+            finish(s - 1)
+        begin(s)
+    finish(seqs - 1)
     all_gone(Q, q_all.at[:len(reach)])
     if paired:
         @pl.when(inner == 1)

time: 49.2 us -> 48.5 us (0.986)
  Pallas kernels: 48.5 us -> 47.7 us
    pallas_call x1, Pallas kernels: 48.5 us -> 47.7 us  [per_device(): pl.pallas_call(functools.partial(heads_kernel, n, n_role, n_seq), out_sha...]
where the time goes in v6:
time: 48.5 us; the launch traced here: 48.3 us
  Pallas kernels  47.7 us (98%)
  local copies, waits for them, and re-layouts  0.6 us (1%)
    pallas_call x1, Pallas kernels, per_device(): pl.pallas_call(functools.partial(heads_kernel, n, n_role, n_seq), out_sha...  47.7 us

profile of v6, /device:TPU:0, one launch (start us, length us, event | category | flops | bytes accessed | tf_op | source)
XLA Modules:
  0.0 48.3 jit_solution(13328585738444388297)
XLA Ops:
  0.0 47.7 %layer.1 = bf16[4,1792]{1,0:T(4,128)(2,1)S(1)} custom-call(bf16[2,64,576]{2,1,0:T(8,128)(2,1)} %bitcast.3, bf16[2,576,1024]{2,1,0:T(8,128)(2,1)} %bitcast.2, s32[2]{0:T(128)} %len_ref.1, s32[4]{0:T(128)} %pos_ref.1, bf16[32,128,128]{2,1,0:T(8,128)(2,1)} %vu_hbm.1, bf16[16,1792]{1,0:T(8,128)(2,1)} %res_hbm.1, f32[1792]{0:T(1024)} %gain_hbm.1, ...), custom_call_target="tpu_custom_call" | custom-call | tf_op jit(solution)/shard_map/layer/pallas_call | solution.py:813
  47.7 0.6 %copy.13 = bf16[4,1792]{1,0:T(4,128)(2,1)} copy(bf16[4,1792]{1,0:T(4,128)(2,1)S(1)} %layer.1) | data formatting | bytes 28672

commit v7 on v6

--- a/solution.py
+++ b/solution.py
@@ -671,9 +671,13 @@
                 total = total + jnp.dot(xv[s, k], wo[wo_rows(k), c0:c1], preferred_element_type=f32)
             po[s, :, c0:c1] = total
             po_send[s, :, c0:c1] = total.astype(bf16)
+            if s == seqs - 1:
+                for k in near[::-1]:
+                    send(po_send.at[s, :, c0:c1], po_recv.at[s, me, :, c0:c1], PO, posem.at[s, p],
+                         {"ctx": k})
+        if s < seqs - 1:
             for k in near[::-1]:
-                send(po_send.at[s, :, c0:c1], po_recv.at[s, me, :, c0:c1], PO, posem.at[s, p],
-                     {"ctx": k})
+                send(po_send.at[s], po_recv.at[s, me], PO, posem.at[s, 0], {"ctx": k})
 
     for s in range(seqs):
         merge(s)
@@ -701,7 +705,10 @@
     sumsq = jnp.zeros((all_rows, 1), f32)
     for p, (c0, c1) in enumerate(parts):
         for s in range(seqs):
-            all_here(po_recv.at[s, :n - 1, :, c0:c1], posem.at[s, p])
+            if s == seqs - 1:
+                all_here(po_recv.at[s, :n - 1, :, c0:c1], posem.at[s, p])
+            elif p == 0:
+                all_here(po_recv.at[s, :n - 1], posem.at[s, 0])
             total = po[s, :, c0:c1]
             for k in near:
                 total = total + po_recv[s, k, :, c0:c1].astype(f32)

time: 48.5 us -> 48.5 us (level)
  no operation moved by 1% of the time
where the time goes in v7:
time: 48.5 us; the launch traced here: 48.3 us
  Pallas kernels  47.7 us (98%)
  local copies, waits for them, and re-layouts  0.6 us (1%)
    pallas_call x1, Pallas kernels, per_device(): pl.pallas_call(functools.partial(heads_kernel, n, n_role, n_seq), out_sha...  47.7 us

profile of v7, /device:TPU:0, one launch (start us, length us, event | category | flops | bytes accessed | tf_op | source)
XLA Modules:
  0.0 48.3 jit_solution(7874797156179874661)
XLA Ops:
  0.0 47.7 %layer.1 = bf16[4,1792]{1,0:T(4,128)(2,1)S(1)} custom-call(bf16[2,64,576]{2,1,0:T(8,128)(2,1)} %bitcast.3, bf16[2,576,1024]{2,1,0:T(8,128)(2,1)} %bitcast.2, s32[2]{0:T(128)} %len_ref.1, s32[4]{0:T(128)} %pos_ref.1, bf16[32,128,128]{2,1,0:T(8,128)(2,1)} %vu_hbm.1, bf16[16,1792]{1,0:T(8,128)(2,1)} %res_hbm.1, f32[1792]{0:T(1024)} %gain_hbm.1, ...), custom_call_target="tpu_custom_call" | custom-call | tf_op jit(solution)/shard_map/layer/pallas_call | solution.py:820
  47.7 0.6 %copy.13 = bf16[4,1792]{1,0:T(4,128)(2,1)} copy(bf16[4,1792]{1,0:T(4,128)(2,1)S(1)} %layer.1) | data formatting | bytes 28672
